TPU v7x, 256 devices: a whole 4x4x8 slice. The times are simulated.
256 devices in a mesh: gx: 4 (over z_lo), gy: 8 (over z_hi, x), gz: 8 (over y, core).
Axes of the slice: x: 4, y: 4, z: 8 (z_hi: 2, z_lo: 4; z = z_hi * 4 + z_lo), core: 2. Of those that a mesh axis runs over, the one named last changes fastest.
Arguments:
- volume: bfloat16 [32, 8, 128, 1024], P(None, 'gx', 'gy', 'gz'), may hold values from -6 to 6
- w_first: bfloat16 [3, 3, 3, 32, 32], replicated, may hold values from -0.21875 to 0.21875
- w_second: bfloat16 [3, 3, 3, 32, 32], replicated, may hold values from -0.21875 to 0.21875
- v_first: bfloat16 [3, 3, 3, 32, 32], replicated, may hold values from -0.21875 to 0.21875
- v_second: bfloat16 [3, 3, 3, 32, 32], replicated, may hold values from -0.21875 to 0.21875
Outputs:
- jv: bfloat16 [32, 8, 128, 1024], P(None, 'gx', 'gy', 'gz')
- gv_first: float32 [3, 3, 3, 32, 32], replicated
- gv_second: float32 [3, 3, 3, 32, 32], replicated
All inputs are finite; a program needn't handle non-finite values.
Results may differ from a plain program's by a relative error of at most 0.005.
Values may be sent and summed in bfloat16 or wider, within the bound.
A program may use at most 64 MiB of HBM per device.

v0:
```python
import math
import jax
import jax.numpy as jnp
from jax import lax
from jax.sharding import PartitionSpec as P


def padded_2(cells, sides, width):
    for axis, dim in sides:
        count = lax.axis_size(axis)
        ends = count - 1
        head = lax.slice_in_dim(cells, 0, width, axis=dim)
        tail = lax.slice_in_dim(cells, cells.shape[dim] - width, cells.shape[dim], axis=dim)
        cells = jnp.concatenate(
            [
                lax.ppermute(tail, axis, [(i, (i + 1) % count) for i in range(ends)]),
                cells,
                lax.ppermute(head, axis, [((i + 1) % count, i) for i in range(ends)]),
            ],
            axis=dim,
        )
    return cells


def gelu_pair(pre):
    inner = 0.7978845608 * (pre + 0.044715 * pre * pre * pre)
    hyper = jnp.tanh(inner)
    hidden = 0.5 * pre * (1.0 + hyper)
    slope = 0.5 * (1.0 + hyper) + 0.5 * pre * (1.0 - hyper * hyper) * 0.7978845608 * (
        1.0 + 0.134145 * pre * pre
    )
    return (hidden, slope)


def stencil(padded, weight):
    depth = padded.shape[1] - 2
    height = padded.shape[2] - 2
    width = padded.shape[3] - 2
    in_chan = weight.shape[3]
    out_chan = weight.shape[4]
    summed = jnp.zeros((out_chan, depth, height, width), jnp.float32)
    for shift_x in range(3):
        for shift_y in range(3):
            stacked = jnp.concatenate(
                [
                    padded[
                        :,
                        shift_x : shift_x + depth,
                        shift_y : shift_y + height,
                        shift_z : shift_z + width,
                    ]
                    for shift_z in range(3)
                ],
                axis=0,
            )
            matrix = weight[shift_x, shift_y].reshape(3 * in_chan, out_chan)
            summed = summed + jnp.einsum(
                "kxyz,ko->oxyz", stacked, matrix, preferred_element_type=jnp.float32
            )
    return summed


def correlate(padded, target):
    depth = target.shape[1]
    height = target.shape[2]
    width = target.shape[3]
    in_chan = padded.shape[0]
    out_chan = target.shape[0]
    planes = []
    for shift_x in range(3):
        rows_y = []
        for shift_y in range(3):
            stacked = jnp.concatenate(
                [
                    padded[
                        :,
                        shift_x : shift_x + depth,
                        shift_y : shift_y + height,
                        shift_z : shift_z + width,
                    ]
                    for shift_z in range(3)
                ],
                axis=0,
            )
            product = jnp.einsum(
                "kxyz,oxyz->ko", stacked, target, preferred_element_type=jnp.float32
            )
            rows_y.append(product.reshape(3, in_chan, out_chan))
        planes.append(jnp.stack(rows_y))
    return jnp.stack(planes)


def body(volume, w_first, w_second, v_first, v_second):
    channels = volume.shape[0]
    depth = volume.shape[1]
    height = volume.shape[2]
    width = volume.shape[3]
    count_all = float(
        depth * height * width * lax.axis_size("gx") * lax.axis_size("gy") * lax.axis_size("gz")
    )
    factor = math.sqrt(27.0 * channels)
    input_pad = padded_2(volume, (("gx", 1), ("gy", 2), ("gz", 3)), 1)
    pre = stencil(input_pad, w_first)
    hidden_f, slope = gelu_pair(pre)
    hidden = hidden_f.astype(jnp.bfloat16)
    tangent = (slope * stencil(input_pad, v_first)).astype(jnp.bfloat16)
    paired = padded_2(jnp.stack([hidden, tangent]), (("gx", 2), ("gy", 3), ("gz", 4)), 1)
    hidden_pad = paired[0]
    tangent_pad = paired[1]
    jv = (stencil(tangent_pad, w_second) + stencil(hidden_pad, v_second)).astype(jnp.bfloat16)
    local_second = correlate(hidden_pad, jv)
    jv_pad = padded_2(jv, (("gx", 1), ("gy", 2), ("gz", 3)), 1)
    flipped = jnp.transpose(jnp.flip(w_second, (0, 1, 2)), (0, 1, 2, 4, 3))
    back = (slope * stencil(jv_pad, flipped)).astype(jnp.bfloat16)
    local_first = correlate(input_pad, back)
    summed_first, summed_second = lax.psum((local_first, local_second), ("gx", "gy", "gz"))
    gv_first = factor * (summed_first / count_all + 0.1 * v_first.astype(jnp.float32))
    gv_second = factor * (summed_second / count_all + 0.1 * v_second.astype(jnp.float32))
    return (jv, gv_first, gv_second)


def solution(mesh):
    in_specs = (P(None, "gx", "gy", "gz"), P(), P(), P(), P())
    out_specs = (P(None, "gx", "gy", "gz"), P(), P())
    return jax.shard_map(body, mesh=mesh, in_specs=in_specs, out_specs=out_specs, check_vma=False)
```

profile of v0, /device:TPU:2, one launch (start us, length us, event | category | flops | bytes accessed | tf_op | source)
XLA Modules:
  0.0 443.7 jit_solution(16340484945520998631)
XLA Ops:
  7.2 1.1 copy.134
  8.4 1.3 collective-permute-start.1
  9.7 4.6 %collective-permute-start = (bf16[32,1,16,128]{3,0,2,1:T(8,128)(2,1)S(1)}, bf16[32,1,16,128]{3,0,2,1:T(8,128)(2,1)S(1)}, u32[]{:S(2)}, u32[]{:S(2)}) collective-permute-start(bf16[32,1,16,128]{3,0,2,1:T(8,128)(2,1)S(1)} %get-tuple-element.141), channel_id=1, source_target_pairs={{0,64},{64,128},{128,192},{1,65},{65,129},{129,193},{2,66},{66,130... | collective-permute-start | bytes 393224 | tf_op jit(solution)/shard_map/ppermute | solution.py:16
  14.2 1.5 fusion.203
  15.8 1.1 collective-permute-done
  17.1 3.4 collective-permute-start.2
  20.5 2.4 collective-permute-start.3
  23.6 2.7 collective-permute-done.3
  26.6 1.1 copy.137
  28.2 1.3 collective-permute-start.5
  29.5 3.0 collective-permute-start.4
  32.7 0.9 collective-permute-done.4
  34.1 1.3 copy.140
  36.2 1.1 fusion.191
  45.1 4.4 collective-permute-start.6
  49.5 1.3 collective-permute-start.7
  51.6 4.3 collective-permute-done.6
  55.9 4.5 %collective-permute-done.7 = bf16[2,32,1,16,128]{4,1,3,2,0:T(8,128)(2,1)S(1)} collective-permute-done((bf16[2,32,1,16,128]{4,1,3,2,0:T(8,128)(2,1)S(1)}, bf16[2,32,1,16,128]{4,1,3,2,0:T(8,128)(2,1)S(1)}, u32[]{:S(2)}, u32[]{:S(2)}) %collective-permute-start.7) | collective-permute-done | bytes 262176 | tf_op jit(solution)/shard_map/ppermute | solution.py:18
  60.5 8.2 %collective-permute-start.8 = (bf16[2,32,4,1,128]{4,1,3,2,0:T(8,128)(2,1)S(1)}, bf16[2,32,4,1,128]{4,1,3,2,0:T(8,128)(2,1)S(1)}, u32[]{:S(2)}, u32[]{:S(2)}) collective-permute-start(bf16[2,32,4,1,128]{4,1,3,2,0:T(8,128)(2,1)S(1)} %get-tuple-element.108), channel_id=1, source_target_pairs={{0,8},{8,16},{16,24},{24,32},{32,40},{40,48},{48,56},{1,9},{9,17},... | collective-permute-start | bytes 196616 | tf_op jit(solution)/shard_map/ppermute | solution.py:16
  68.7 1.9 collective-permute-start.9
  71.3 9.5 %collective-permute-done.9 = bf16[2,32,4,1,128]{4,1,3,2,0:T(8,128)(2,1)S(1)} collective-permute-done((bf16[2,32,4,1,128]{4,1,3,2,0:T(8,128)(2,1)S(1)}, bf16[2,32,4,1,128]{4,1,3,2,0:T(8,128)(2,1)S(1)}, u32[]{:S(2)}, u32[]{:S(2)}) %collective-permute-start.9) | collective-permute-done | bytes 65568 | tf_op jit(solution)/shard_map/ppermute | solution.py:18
  82.3 1.5 copy.162
  83.9 0.9 copy.163
  84.8 1.3 collective-permute-start.11
  86.1 3.2 collective-permute-start.10
  89.3 1.6 fusion.201
  96.1 1.0 copy.164
  97.1 1.7 copy.165
  98.8 3.8 pad_maximum_fusion
  103.4 1.2 fusion.188
  105.1 1.2 fusion.186
  117.3 2.9 collective-permute-start.12
  120.3 1.3 collective-permute-start.13
  122.0 1.9 collective-permute-done.12
  123.9 4.5 %collective-permute-done.13 = bf16[32,1,16,128]{3,0,2,1:T(8,128)(2,1)S(1)} collective-permute-done((bf16[32,1,16,128]{3,0,2,1:T(8,128)(2,1)S(1)}, bf16[32,1,16,128]{3,0,2,1:T(8,128)(2,1)S(1)}, u32[]{:S(2)}, u32[]{:S(2)}) %collective-permute-start.13) | collective-permute-done | bytes 131104 | tf_op jit(solution)/shard_map/ppermute | solution.py:18
  128.5 3.9 collective-permute-start.14
  132.4 2.1 collective-permute-start.15
  134.6 1.0 pad_maximum_fusion.27
  135.6 7.3 %collective-permute-done.15 = bf16[32,4,1,128]{3,0,2,1:T(8,128)(2,1)S(1)} collective-permute-done((bf16[32,4,1,128]{3,0,2,1:T(8,128)(2,1)S(1)}, bf16[32,4,1,128]{3,0,2,1:T(8,128)(2,1)S(1)}, u32[]{:S(2)}, u32[]{:S(2)}) %collective-permute-start.15) | collective-permute-done | bytes 32800 | tf_op jit(solution)/shard_map/ppermute | solution.py:18
  144.2 1.3 collective-permute-start.17
  145.5 3.0 collective-permute-start.16
  148.8 0.9 fusion.196
  150.8 1.4 maximum_maximum_fusion.1
  168.3 1.0 pad_maximum_fusion.26
  170.5 262.7 %all-reduce.3.cloned.1.call-done = (f32[3,3,3,32,32]{3,2,4,1,0:T(4,128)}, f32[3,3,3,32,32]{3,2,4,1,0:T(4,128)}) async-done(((f32[3,3,3,32,32]{3,2,4,1,0:T(4,128)}, f32[3,3,3,32,32]{3,2,4,1,0:T(4,128)}), (f32[3,3,3,32,32]{3,2,4,1,0:T(4,128)}, f32[3,3,3,32,32]{3,2,4,1,0:T(4,128)})) %all-reduce.3.cloned.1.call-update) | async-done | bytes 221200 | tf_op jit(solution)/shard_map/psum | solution.py:116
  433.2 1.4 add_multiply_fusion.1
  434.6 1.0 copy.200
  435.9 1.0 copy.201
  (369 shorter events, 50.9 us)
Async XLA Ops:
  7.2 9.7 %copy-start.2 = (bf16[32,2,16,128]{3,2,1,0:T(8,128)(2,1)S(1)}, bf16[32,2,16,128]{3,2,1,0:T(8,128)(2,1)}, u32[]{:S(2)}) copy-start(bf16[32,2,16,128]{3,2,1,0:T(8,128)(2,1)} %param.5) | copy-start | bytes 786436
  7.2 15.8 %copy-start.6 = (bf16[3,3,3,32,32]{4,3,2,1,0:T(8,128)(2,1)S(1)}, bf16[3,3,3,32,32]{4,3,2,1,0:T(8,128)(2,1)}, u32[]{:S(2)}) copy-start(bf16[3,3,3,32,32]{4,3,2,1,0:T(8,128)(2,1)} %param.8) | copy-start | bytes 165892
  7.2 426.0 %all-reduce.3.cloned.1.call-start = ((), (), s32[]{:S(2)}) async-start(), calls=%async_computation | async-start | bytes 2359296 | tf_op jit(solution)/shard_map/psum | solution.py:116
  8.3 35.9 %copy-start.3 = (bf16[32,2,16,128]{3,0,2,1:T(8,128)(2,1)}, bf16[32,2,16,128]{3,0,2,1:T(8,128)(2,1)S(1)}, u32[]{:S(2)}) copy-start(bf16[32,2,16,128]{3,0,2,1:T(8,128)(2,1)S(1)} %copy.134) | copy-start | bytes 786436
  8.4 8.6 %collective-permute-start.1 = (bf16[32,1,16,128]{3,0,2,1:T(8,128)(2,1)S(1)}, bf16[32,1,16,128]{3,0,2,1:T(8,128)(2,1)S(1)}, u32[]{:S(2)}, u32[]{:S(2)}) collective-permute-start(bf16[32,1,16,128]{3,0,2,1:T(8,128)(2,1)S(1)} %get-tuple-element.140), channel_id=1, source_target_pairs={{64,0},{128,64},{192,128},{65,1},{129,65},{193,129},{66,2},{130,66... | collective-permute-start | bytes 393224 | tf_op jit(solution)/shard_map/ppermute | solution.py:18
  9.7 7.2 %collective-permute-start = (bf16[32,1,16,128]{3,0,2,1:T(8,128)(2,1)S(1)}, bf16[32,1,16,128]{3,0,2,1:T(8,128)(2,1)S(1)}, u32[]{:S(2)}, u32[]{:S(2)}) collective-permute-start(bf16[32,1,16,128]{3,0,2,1:T(8,128)(2,1)S(1)} %get-tuple-element.141), channel_id=1, source_target_pairs={{0,64},{64,128},{128,192},{1,65},{65,129},{129,193},{2,66},{66,130... | collective-permute-start | bytes 393224 | tf_op jit(solution)/shard_map/ppermute | solution.py:16
  16.9 24.9 %copy-start.61 = (bf16[32,1,16,128]{3,0,2,1:T(8,128)(2,1)}, bf16[32,1,16,128]{3,0,2,1:T(8,128)(2,1)S(1)}, u32[]{:S(2)}) copy-start(bf16[32,1,16,128]{3,0,2,1:T(8,128)(2,1)S(1)} %collective-permute-done) | copy-start | bytes 393220
  17.0 27.2 %copy-start.59 = (bf16[32,1,16,128]{3,0,2,1:T(8,128)(2,1)}, bf16[32,1,16,128]{3,0,2,1:T(8,128)(2,1)S(1)}, u32[]{:S(2)}) copy-start(bf16[32,1,16,128]{3,0,2,1:T(8,128)(2,1)S(1)} %collective-permute-done.1) | copy-start | bytes 393220
  17.1 6.5 %collective-permute-start.2 = (bf16[32,4,1,128]{3,0,2,1:T(8,128)(2,1)S(1)}, bf16[32,4,1,128]{3,0,2,1:T(8,128)(2,1)S(1)}, u32[]{:S(2)}, u32[]{:S(2)}) collective-permute-start(bf16[32,4,1,128]{3,0,2,1:T(8,128)(2,1)S(1)} %get-tuple-element.136), channel_id=1, source_target_pairs={{0,8},{8,16},{16,24},{24,32},{32,40},{40,48},{48,56},{1,9},{9,17},... | collective-permute-start | bytes 98312 | tf_op jit(solution)/shard_map/ppermute | solution.py:16
  20.5 5.8 %collective-permute-start.3 = (bf16[32,4,1,128]{3,0,2,1:T(8,128)(2,1)S(1)}, bf16[32,4,1,128]{3,0,2,1:T(8,128)(2,1)S(1)}, u32[]{:S(2)}, u32[]{:S(2)}) collective-permute-start(bf16[32,4,1,128]{3,0,2,1:T(8,128)(2,1)S(1)} %get-tuple-element.137), channel_id=1, source_target_pairs={{8,0},{16,8},{24,16},{32,24},{40,32},{48,40},{56,48},{9,1},{17,9},... | collective-permute-start | bytes 98312 | tf_op jit(solution)/shard_map/ppermute | solution.py:18
  28.2 5.9 %collective-permute-start.5 = (bf16[32,4,18,1]{0,1,3,2:T(4,128)(2,1)S(1)}, bf16[32,4,18,1]{0,1,3,2:T(4,128)(2,1)}, u32[]{:S(2)}, u32[]{:S(2)}) collective-permute-start(bf16[32,4,18,1]{0,1,3,2:T(4,128)(2,1)S(1)} %copy.139), channel_id=1, source_target_pairs={{1,0},{2,1},{3,2},{4,3},{5,4},{6,5},{7,6},{9,8},{10,9},{11,10},{12... | collective-permute-start | bytes 13832 | tf_op jit(solution)/shard_map/ppermute | solution.py:18
  29.5 4.1 collective-permute-start.4
  32.6 8.6 %copy-start.13 = (bf16[32,2,16,128]{3,0,2,1:T(8,128)(2,1)}, bf16[32,2,16,128]{3,0,2,1:T(8,128)(2,1)S(1)}, u32[]{:S(2)}) copy-start(bf16[32,2,16,128]{3,0,2,1:T(8,128)(2,1)S(1)} %get-tuple-element.134) | copy-start | bytes 786436
  32.7 9.5 %copy-start.15 = (bf16[32,2,16,128]{3,0,2,1:T(8,128)(2,1)}, bf16[32,2,16,128]{3,0,2,1:T(8,128)(2,1)S(1)}, u32[]{:S(2)}) copy-start(bf16[32,2,16,128]{3,0,2,1:T(8,128)(2,1)S(1)} %get-tuple-element.125) | copy-start | bytes 786436
  32.7 10.2 %copy-start.17 = (bf16[32,2,16,128]{3,0,2,1:T(8,128)(2,1)}, bf16[32,2,16,128]{3,0,2,1:T(8,128)(2,1)S(1)}, u32[]{:S(2)}) copy-start(bf16[32,2,16,128]{3,0,2,1:T(8,128)(2,1)S(1)} %get-tuple-element.135) | copy-start | bytes 786436
  32.7 10.9 %copy-start.23 = (bf16[32,2,16,128]{3,0,2,1:T(8,128)(2,1)}, bf16[32,2,16,128]{3,0,2,1:T(8,128)(2,1)S(1)}, u32[]{:S(2)}) copy-start(bf16[32,2,16,128]{3,0,2,1:T(8,128)(2,1)S(1)} %get-tuple-element.124) | copy-start | bytes 786436
  37.4 6.1 %copy-start.53 = (bf16[32,2,16,128]{3,0,2,1:T(8,128)(2,1)}, bf16[32,2,16,128]{3,0,2,1:T(8,128)(2,1)S(1)}, u32[]{:S(2)}) copy-start(bf16[32,2,16,128]{3,0,2,1:T(8,128)(2,1)S(1)} %get-tuple-element.93) | copy-start | bytes 786436
  37.4 6.1 %copy-start.55 = (bf16[32,2,16,128]{3,0,2,1:T(8,128)(2,1)}, bf16[32,2,16,128]{3,0,2,1:T(8,128)(2,1)S(1)}, u32[]{:S(2)}) copy-start(bf16[32,2,16,128]{3,0,2,1:T(8,128)(2,1)S(1)} %get-tuple-element.192) | copy-start | bytes 786436
  37.5 6.4 %copy-start.33 = (bf16[32,2,16,128]{3,0,2,1:T(8,128)(2,1)}, bf16[32,2,16,128]{3,0,2,1:T(8,128)(2,1)S(1)}, u32[]{:S(2)}) copy-start(bf16[32,2,16,128]{3,0,2,1:T(8,128)(2,1)S(1)} %get-tuple-element.92) | copy-start | bytes 786436
  37.5 6.4 %copy-start.35 = (bf16[32,2,16,128]{3,0,2,1:T(8,128)(2,1)}, bf16[32,2,16,128]{3,0,2,1:T(8,128)(2,1)S(1)}, u32[]{:S(2)}) copy-start(bf16[32,2,16,128]{3,0,2,1:T(8,128)(2,1)S(1)} %get-tuple-element.193) | copy-start | bytes 786436
  37.5 6.8 %copy-start.19 = (bf16[32,2,16,128]{3,0,2,1:T(8,128)(2,1)}, bf16[32,2,16,128]{3,0,2,1:T(8,128)(2,1)S(1)}, u32[]{:S(2)}) copy-start(bf16[32,2,16,128]{3,0,2,1:T(8,128)(2,1)S(1)} %get-tuple-element.91) | copy-start | bytes 786436
  37.5 6.8 %copy-start.21 = (bf16[32,2,16,128]{3,0,2,1:T(8,128)(2,1)}, bf16[32,2,16,128]{3,0,2,1:T(8,128)(2,1)S(1)}, u32[]{:S(2)}) copy-start(bf16[32,2,16,128]{3,0,2,1:T(8,128)(2,1)S(1)} %get-tuple-element.194) | copy-start | bytes 786436
  37.5 7.0 %copy-start.29 = (bf16[32,2,16,128]{3,0,2,1:T(8,128)(2,1)}, bf16[32,2,16,128]{3,0,2,1:T(8,128)(2,1)S(1)}, u32[]{:S(2)}) copy-start(bf16[32,2,16,128]{3,0,2,1:T(8,128)(2,1)S(1)} %get-tuple-element.90) | copy-start | bytes 786436
  37.5 7.0 %copy-start.31 = (bf16[32,2,16,128]{3,0,2,1:T(8,128)(2,1)}, bf16[32,2,16,128]{3,0,2,1:T(8,128)(2,1)S(1)}, u32[]{:S(2)}) copy-start(bf16[32,2,16,128]{3,0,2,1:T(8,128)(2,1)S(1)} %get-tuple-element.195) | copy-start | bytes 786436
  44.6 6.3 %copy-start.5 = (bf16[3,3,3,32,32]{4,3,2,1,0:T(8,128)(2,1)S(1)}, bf16[3,3,3,32,32]{4,3,2,1,0:T(8,128)(2,1)}, u32[]{:S(2)}) copy-start(bf16[3,3,3,32,32]{4,3,2,1,0:T(8,128)(2,1)} %param.7) | copy-start | bytes 165892
  45.1 10.8 %collective-permute-start.6 = (bf16[2,32,1,16,128]{4,1,3,2,0:T(8,128)(2,1)S(1)}, bf16[2,32,1,16,128]{4,1,3,2,0:T(8,128)(2,1)S(1)}, u32[]{:S(2)}, u32[]{:S(2)}) collective-permute-start(bf16[2,32,1,16,128]{4,1,3,2,0:T(8,128)(2,1)S(1)} %get-tuple-element.132), channel_id=1, source_target_pairs={{0,64},{64,128},{128,192},{1,65},{65,129},{129,193},{2,66},{66,130... | collective-permute-start | bytes 786440 | tf_op jit(solution)/shard_map/ppermute | solution.py:16
  49.5 10.9 %collective-permute-start.7 = (bf16[2,32,1,16,128]{4,1,3,2,0:T(8,128)(2,1)S(1)}, bf16[2,32,1,16,128]{4,1,3,2,0:T(8,128)(2,1)S(1)}, u32[]{:S(2)}, u32[]{:S(2)}) collective-permute-start(bf16[2,32,1,16,128]{4,1,3,2,0:T(8,128)(2,1)S(1)} %get-tuple-element.133), channel_id=1, source_target_pairs={{64,0},{128,64},{192,128},{65,1},{129,65},{193,129},{66,2},{130,66... | collective-permute-start | bytes 786440 | tf_op jit(solution)/shard_map/ppermute | solution.py:18
  55.9 24.9 %copy-start = (bf16[2,32,1,16,128]{4,1,3,2,0:T(8,128)(2,1)}, bf16[2,32,1,16,128]{4,1,3,2,0:T(8,128)(2,1)S(1)}, u32[]{:S(2)}) copy-start(bf16[2,32,1,16,128]{4,1,3,2,0:T(8,128)(2,1)S(1)} %collective-permute-done.6) | copy-start | bytes 786436
  60.5 20.4 %copy-start.1 = (bf16[2,32,1,16,128]{4,1,3,2,0:T(8,128)(2,1)}, bf16[2,32,1,16,128]{4,1,3,2,0:T(8,128)(2,1)S(1)}, u32[]{:S(2)}) copy-start(bf16[2,32,1,16,128]{4,1,3,2,0:T(8,128)(2,1)S(1)} %collective-permute-done.7) | copy-start | bytes 786436
  60.5 10.8 %collective-permute-start.8 = (bf16[2,32,4,1,128]{4,1,3,2,0:T(8,128)(2,1)S(1)}, bf16[2,32,4,1,128]{4,1,3,2,0:T(8,128)(2,1)S(1)}, u32[]{:S(2)}, u32[]{:S(2)}) collective-permute-start(bf16[2,32,4,1,128]{4,1,3,2,0:T(8,128)(2,1)S(1)} %get-tuple-element.108), channel_id=1, source_target_pairs={{0,8},{8,16},{16,24},{24,32},{32,40},{40,48},{48,56},{1,9},{9,17},... | collective-permute-start | bytes 196616 | tf_op jit(solution)/shard_map/ppermute | solution.py:16
  68.7 12.2 %collective-permute-start.9 = (bf16[2,32,4,1,128]{4,1,3,2,0:T(8,128)(2,1)S(1)}, bf16[2,32,4,1,128]{4,1,3,2,0:T(8,128)(2,1)S(1)}, u32[]{:S(2)}, u32[]{:S(2)}) collective-permute-start(bf16[2,32,4,1,128]{4,1,3,2,0:T(8,128)(2,1)S(1)} %get-tuple-element.109), channel_id=1, source_target_pairs={{8,0},{16,8},{24,16},{32,24},{40,32},{48,40},{56,48},{9,1},{17,9},... | collective-permute-start | bytes 196616 | tf_op jit(solution)/shard_map/ppermute | solution.py:18
  83.8 7.1 %copy-start.72 = (bf16[1,1,3,32,32]{3,4,2,1,0:T(8,128)(2,1)S(1)}, bf16[1,1,3,32,32]{3,4,2,1,0:T(8,128)(2,1)}, u32[]{:S(2)}) copy-start(bf16[1,1,3,32,32]{3,4,2,1,0:T(8,128)(2,1)} %get-tuple-element.142) | copy-start | bytes 18436
  83.8 7.2 %copy-start.71 = (bf16[1,1,3,32,32]{3,4,2,1,0:T(8,128)(2,1)S(1)}, bf16[1,1,3,32,32]{3,4,2,1,0:T(8,128)(2,1)}, u32[]{:S(2)}) copy-start(bf16[1,1,3,32,32]{3,4,2,1,0:T(8,128)(2,1)} %get-tuple-element.143) | copy-start | bytes 18436
  83.8 7.3 %copy-start.70 = (bf16[1,1,3,32,32]{3,4,2,1,0:T(8,128)(2,1)S(1)}, bf16[1,1,3,32,32]{3,4,2,1,0:T(8,128)(2,1)}, u32[]{:S(2)}) copy-start(bf16[1,1,3,32,32]{3,4,2,1,0:T(8,128)(2,1)} %get-tuple-element.144) | copy-start | bytes 18436
  83.8 8.0 %copy-start.69 = (bf16[1,1,3,32,32]{3,4,2,1,0:T(8,128)(2,1)S(1)}, bf16[1,1,3,32,32]{3,4,2,1,0:T(8,128)(2,1)}, u32[]{:S(2)}) copy-start(bf16[1,1,3,32,32]{3,4,2,1,0:T(8,128)(2,1)} %get-tuple-element.145) | copy-start | bytes 18436
  83.8 8.7 %copy-start.68 = (bf16[1,1,3,32,32]{3,4,2,1,0:T(8,128)(2,1)S(1)}, bf16[1,1,3,32,32]{3,4,2,1,0:T(8,128)(2,1)}, u32[]{:S(2)}) copy-start(bf16[1,1,3,32,32]{3,4,2,1,0:T(8,128)(2,1)} %get-tuple-element.146) | copy-start | bytes 18436
  83.8 9.4 %copy-start.67 = (bf16[1,1,3,32,32]{3,4,2,1,0:T(8,128)(2,1)S(1)}, bf16[1,1,3,32,32]{3,4,2,1,0:T(8,128)(2,1)}, u32[]{:S(2)}) copy-start(bf16[1,1,3,32,32]{3,4,2,1,0:T(8,128)(2,1)} %get-tuple-element.147) | copy-start | bytes 18436
  83.8 10.1 %copy-start.66 = (bf16[1,1,3,32,32]{3,4,2,1,0:T(8,128)(2,1)S(1)}, bf16[1,1,3,32,32]{3,4,2,1,0:T(8,128)(2,1)}, u32[]{:S(2)}) copy-start(bf16[1,1,3,32,32]{3,4,2,1,0:T(8,128)(2,1)} %get-tuple-element.148) | copy-start | bytes 18436
  83.8 10.8 %copy-start.65 = (bf16[1,1,3,32,32]{3,4,2,1,0:T(8,128)(2,1)S(1)}, bf16[1,1,3,32,32]{3,4,2,1,0:T(8,128)(2,1)}, u32[]{:S(2)}) copy-start(bf16[1,1,3,32,32]{3,4,2,1,0:T(8,128)(2,1)} %get-tuple-element.149) | copy-start | bytes 18436
  83.8 11.5 %copy-start.64 = (bf16[1,1,3,32,32]{3,4,2,1,0:T(8,128)(2,1)S(1)}, bf16[1,1,3,32,32]{3,4,2,1,0:T(8,128)(2,1)}, u32[]{:S(2)}) copy-start(bf16[1,1,3,32,32]{3,4,2,1,0:T(8,128)(2,1)} %get-tuple-element.150) | copy-start | bytes 18436
  84.8 12.3 %collective-permute-start.11 = (bf16[2,32,4,18,1]{1,2,4,3,0:T(4,128)(2,1)S(1)}, bf16[2,32,4,18,1]{1,2,4,3,0:T(4,128)(2,1)}, u32[]{:S(2)}, u32[]{:S(2)}) collective-permute-start(bf16[2,32,4,18,1]{1,2,4,3,0:T(4,128)(2,1)S(1)} %copy.163), channel_id=1, source_target_pairs={{1,0},{2,1},{3,2},{4,3},{5,4},{6,5},{7,6},{9,8},{10,9},{11,10},{12... | collective-permute-start | bytes 27656 | tf_op jit(solution)/shard_map/ppermute | solution.py:18
  86.1 10.0 %collective-permute-start.10 = (bf16[2,32,4,18,1]{1,2,4,3,0:T(4,128)(2,1)}, bf16[2,32,4,18,1]{1,2,4,3,0:T(4,128)(2,1)S(1)}, u32[]{:S(2)}, u32[]{:S(2)}) collective-permute-start(bf16[2,32,4,18,1]{1,2,4,3,0:T(4,128)(2,1)} %copy.162), channel_id=1, source_target_pairs={{0,1},{1,2},{2,3},{3,4},{4,5},{5,6},{6,7},{8,9},{9,10},{10,11},{11... | collective-permute-start | bytes 27656 | tf_op jit(solution)/shard_map/ppermute | solution.py:16
  117.3 6.6 %collective-permute-start.12 = (bf16[32,1,16,128]{3,0,2,1:T(8,128)(2,1)S(1)}, bf16[32,1,16,128]{3,0,2,1:T(8,128)(2,1)S(1)}, u32[]{:S(2)}, u32[]{:S(2)}) collective-permute-start(bf16[32,1,16,128]{3,0,2,1:T(8,128)(2,1)S(1)} %get-tuple-element.138), channel_id=1, source_target_pairs={{0,64},{64,128},{128,192},{1,65},{65,129},{129,193},{2,66},{66,130... | collective-permute-start | bytes 393224 | tf_op jit(solution)/shard_map/ppermute | solution.py:16
  120.3 8.2 %collective-permute-start.13 = (bf16[32,1,16,128]{3,0,2,1:T(8,128)(2,1)S(1)}, bf16[32,1,16,128]{3,0,2,1:T(8,128)(2,1)S(1)}, u32[]{:S(2)}, u32[]{:S(2)}) collective-permute-start(bf16[32,1,16,128]{3,0,2,1:T(8,128)(2,1)S(1)} %get-tuple-element.139), channel_id=1, source_target_pairs={{64,0},{128,64},{192,128},{65,1},{129,65},{193,129},{66,2},{130,66... | collective-permute-start | bytes 393224 | tf_op jit(solution)/shard_map/ppermute | solution.py:18
  128.5 7.1 %collective-permute-start.14 = (bf16[32,4,1,128]{3,0,2,1:T(8,128)(2,1)S(1)}, bf16[32,4,1,128]{3,0,2,1:T(8,128)(2,1)S(1)}, u32[]{:S(2)}, u32[]{:S(2)}) collective-permute-start(bf16[32,4,1,128]{3,0,2,1:T(8,128)(2,1)S(1)} %get-tuple-element.130), channel_id=1, source_target_pairs={{0,8},{8,16},{16,24},{24,32},{32,40},{40,48},{48,56},{1,9},{9,17},... | collective-permute-start | bytes 98312 | tf_op jit(solution)/shard_map/ppermute | solution.py:16
  132.4 10.5 %collective-permute-start.15 = (bf16[32,4,1,128]{3,0,2,1:T(8,128)(2,1)S(1)}, bf16[32,4,1,128]{3,0,2,1:T(8,128)(2,1)S(1)}, u32[]{:S(2)}, u32[]{:S(2)}) collective-permute-start(bf16[32,4,1,128]{3,0,2,1:T(8,128)(2,1)S(1)} %get-tuple-element.131), channel_id=1, source_target_pairs={{8,0},{16,8},{24,16},{32,24},{40,32},{48,40},{56,48},{9,1},{17,9},... | collective-permute-start | bytes 98312 | tf_op jit(solution)/shard_map/ppermute | solution.py:18
  144.2 6.0 %collective-permute-start.17 = (bf16[32,4,18,1]{0,1,3,2:T(4,128)(2,1)S(1)}, bf16[32,4,18,1]{0,1,3,2:T(4,128)(2,1)S(1)}, u32[]{:S(2)}, u32[]{:S(2)}) collective-permute-start(bf16[32,4,18,1]{0,1,3,2:T(4,128)(2,1)S(1)} %copy.186), channel_id=1, source_target_pairs={{1,0},{2,1},{3,2},{4,3},{5,4},{6,5},{7,6},{9,8},{10,9},{11,10},{12... | collective-permute-start | bytes 13832 | tf_op jit(solution)/shard_map/ppermute | solution.py:18
  145.5 4.2 collective-permute-start.16
  (78 other events, 114.0 us)
Sparse Core Ops, SparseCore 0:
  169.4 263.7 all-reduce.2
where the time goes:
time: 446 us; the launch traced here: 444 us
  waiting for transfers between devices  300 us (67%)
  starting transfers between devices  51 us (11%)
  local copies, waits for them, and re-layouts  47.2 us (11%)
  matrix products  19.3 us (4%)
  between operations  15.8 us (4%)
  other arithmetic  10.9 us (2%)
    psum x1, waiting for transfers between devices, body(): lax.psum((local_first, local_second), ('gx', 'gy', 'gz'))  263 us
    ppermute x9, starting transfers between devices, padded_2(): lax.ppermute(tail, axis, [(i, (i + 1) % count) for i in range(ends)])  36.7 us
    ppermute x9, waiting for transfers between devices, padded_2(): lax.ppermute(head, axis, [((i + 1) % count, i) for i in range(ends)])  28.6 us
    unnamed x222, local copies, waits for them, and re-layouts  16.6 us
    ppermute x9, starting transfers between devices, padded_2(): lax.ppermute(head, axis, [((i + 1) % count, i) for i in range(ends)])  14.2 us
    dot_general x45, matrix products, stencil(): jnp.einsum('kxyz,ko->oxyz', stacked, matrix, preferred_element_type=jnp.f...  12.7 us
  transfers between devices with their start and end apart: 19, of which 10 were waited for; matrix products, arithmetic and copies ran while one was open for 4% of the time, Pallas kernels for 0%

commit v1 on v0

--- a/solution.py
+++ b/solution.py
@@ -113,7 +113,9 @@
     flipped = jnp.transpose(jnp.flip(w_second, (0, 1, 2)), (0, 1, 2, 4, 3))
     back = (slope * stencil(jv_pad, flipped)).astype(jnp.bfloat16)
     local_first = correlate(input_pad, back)
-    summed_first, summed_second = lax.psum((local_first, local_second), ("gx", "gy", "gz"))
+    summed_first, summed_second = lax.psum(
+        lax.psum((local_first, local_second), "gx"), ("gy", "gz")
+    )
     gv_first = factor * (summed_first / count_all + 0.1 * v_first.astype(jnp.float32))
     gv_second = factor * (summed_second / count_all + 0.1 * v_second.astype(jnp.float32))
     return (jv, gv_first, gv_second)

time: 446 us -> 1020 us (2.29)
  the two profiles are of different devices: /device:TPU:2 before, /device:TPU:32 now
where the time goes in v1:
time: 1020 us
  waiting for transfers between devices  878 us (86%)
  starting transfers between devices  50 us (5%)
  local copies, waits for them, and re-layouts  47.2 us (5%)
  matrix products  19.3 us (2%)
  between operations  15.8 us (2%)
  other arithmetic  10.9 us (1%)
    psum x1, waiting for transfers between devices, body(): lax.psum(lax.psum((local_first, local_second), 'gx'), ('gy', 'gz'))  772 us
    psum x1, waiting for transfers between devices, body(): lax.psum((local_first, local_second), 'gx')  74.3 us
    ppermute x9, starting transfers between devices, padded_2(): lax.ppermute(tail, axis, [(i, (i + 1) % count) for i in range(ends)])  33.3 us
    ppermute x9, waiting for transfers between devices, padded_2(): lax.ppermute(head, axis, [((i + 1) % count, i) for i in range(ends)])  21.7 us
  transfers between devices with their start and end apart: 20, of which 11 were waited for; matrix products, arithmetic and copies ran while one was open for 2% of the time, Pallas kernels for 0%

profile of v1, /device:TPU:32, one launch (start us, length us, event | category | flops | bytes accessed | tf_op | source)
XLA Modules:
  0.0 1021.6 jit_solution(3891689551164280670)
XLA Ops:
  7.2 1.1 copy.134
  8.4 3.7 collective-permute-start.1
  12.1 2.1 collective-permute-start
  14.2 1.5 fusion.203
  15.7 3.2 collective-permute-done
  19.2 1.9 collective-permute-start.2
  21.0 1.3 collective-permute-start.3
  23.0 3.8 collective-permute-done.3
  27.2 1.1 copy.137
  28.8 1.3 collective-permute-start.5
  30.1 3.0 collective-permute-start.4
  33.2 0.9 collective-permute-done.4
  34.7 1.3 copy.140
  36.8 1.1 fusion.191
  45.7 3.8 collective-permute-start.6
  49.5 2.0 collective-permute-start.7
  52.3 4.2 collective-permute-done.6
  56.5 4.1 collective-permute-done.7
  60.6 3.4 collective-permute-start.8
  64.0 1.3 collective-permute-start.9
  66.1 7.3 collective-permute-done.9
  74.8 1.5 copy.162
  76.4 0.9 copy.163
  77.3 1.3 collective-permute-start.11
  78.6 3.2 collective-permute-start.10
  81.9 1.6 fusion.201
  88.6 1.0 copy.164
  89.6 1.7 copy.165
  91.3 3.8 pad_maximum_fusion
  96.0 1.2 fusion.188
  97.6 1.2 fusion.186
  109.9 2.9 collective-permute-start.12
  112.8 2.9 collective-permute-start.13
  116.2 1.7 collective-permute-done.12
  117.9 3.1 collective-permute-done.13
  121.0 9.9 collective-permute-start.14
  131.0 1.5 collective-permute-start.15
  132.5 1.0 pad_maximum_fusion.27
  133.5 3.3 collective-permute-done.15
  138.1 1.3 collective-permute-start.17
  139.4 3.0 collective-permute-start.16
  144.7 1.4 maximum_maximum_fusion.1
  162.2 1.0 pad_maximum_fusion.26
  163.2 74.3 %all-reduce.7.cloned.1.call-done = (f32[3,3,3,32,32]{3,2,4,1,0:T(4,128)}, f32[3,3,3,32,32]{3,2,4,1,0:T(4,128)}) async-done(((f32[3,3,3,32,32]{3,2,4,1,0:T(4,128)}, f32[3,3,3,32,32]{3,2,4,1,0:T(4,128)}), (f32[3,3,3,32,32]{3,2,4,1,0:T(4,128)}, f32[3,3,3,32,32]{3,2,4,1,0:T(4,128)})) %all-reduce.7.cloned.1.call-update) | async-done | bytes 221200 | tf_op jit(solution)/shard_map/psum | solution.py:117
  238.8 772.3 %all-reduce.5.cloned.1.call-done = (f32[3,3,3,32,32]{3,2,4,1,0:T(4,128)}, f32[3,3,3,32,32]{3,2,4,1,0:T(4,128)}) async-done(((f32[3,3,3,32,32]{3,2,4,1,0:T(4,128)}, f32[3,3,3,32,32]{3,2,4,1,0:T(4,128)}), (f32[3,3,3,32,32]{3,2,4,1,0:T(4,128)}, f32[3,3,3,32,32]{3,2,4,1,0:T(4,128)})) %all-reduce.5.cloned.1.call-update) | async-done | bytes 221200 | tf_op jit(solution)/shard_map/psum | solution.py:116
  1011.1 1.4 add_multiply_fusion.1
  1012.6 1.0 copy.200
  1013.8 1.0 copy.201
  (372 shorter events, 51.9 us)
Async XLA Ops:
  7.2 11.8 %copy-start.2 = (bf16[32,2,16,128]{3,2,1,0:T(8,128)(2,1)S(1)}, bf16[32,2,16,128]{3,2,1,0:T(8,128)(2,1)}, u32[]{:S(2)}) copy-start(bf16[32,2,16,128]{3,2,1,0:T(8,128)(2,1)} %param.5) | copy-start | bytes 786436
  7.2 15.2 %copy-start.6 = (bf16[3,3,3,32,32]{4,3,2,1,0:T(8,128)(2,1)S(1)}, bf16[3,3,3,32,32]{4,3,2,1,0:T(8,128)(2,1)}, u32[]{:S(2)}) copy-start(bf16[3,3,3,32,32]{4,3,2,1,0:T(8,128)(2,1)} %param.8) | copy-start | bytes 165892
  7.2 230.3 %all-reduce.7.cloned.1.call-start = ((), (), s32[]{:S(2)}) async-start(), calls=%async_computation.1 | async-start | bytes 2359296 | tf_op jit(solution)/shard_map/psum | solution.py:117
  8.3 36.4 %copy-start.3 = (bf16[32,2,16,128]{3,0,2,1:T(8,128)(2,1)}, bf16[32,2,16,128]{3,0,2,1:T(8,128)(2,1)S(1)}, u32[]{:S(2)}) copy-start(bf16[32,2,16,128]{3,0,2,1:T(8,128)(2,1)S(1)} %copy.134) | copy-start | bytes 786436
  8.4 10.7 %collective-permute-start.1 = (bf16[32,1,16,128]{3,0,2,1:T(8,128)(2,1)S(1)}, bf16[32,1,16,128]{3,0,2,1:T(8,128)(2,1)S(1)}, u32[]{:S(2)}, u32[]{:S(2)}) collective-permute-start(bf16[32,1,16,128]{3,0,2,1:T(8,128)(2,1)S(1)} %get-tuple-element.142), channel_id=1, source_target_pairs={{64,0},{128,64},{192,128},{65,1},{129,65},{193,129},{66,2},{130,66... | collective-permute-start | bytes 393224 | tf_op jit(solution)/shard_map/ppermute | solution.py:18
  12.1 6.9 collective-permute-start
  19.0 23.4 %copy-start.61 = (bf16[32,1,16,128]{3,0,2,1:T(8,128)(2,1)}, bf16[32,1,16,128]{3,0,2,1:T(8,128)(2,1)S(1)}, u32[]{:S(2)}) copy-start(bf16[32,1,16,128]{3,0,2,1:T(8,128)(2,1)S(1)} %collective-permute-done) | copy-start | bytes 393220
  19.1 25.7 %copy-start.59 = (bf16[32,1,16,128]{3,0,2,1:T(8,128)(2,1)}, bf16[32,1,16,128]{3,0,2,1:T(8,128)(2,1)S(1)}, u32[]{:S(2)}) copy-start(bf16[32,1,16,128]{3,0,2,1:T(8,128)(2,1)S(1)} %collective-permute-done.1) | copy-start | bytes 393220
  19.2 3.9 collective-permute-start.2
  21.0 5.8 collective-permute-start.3
  28.8 5.9 collective-permute-start.5
  30.1 4.1 collective-permute-start.4
  33.2 8.6 copy-start.13
  33.2 9.5 copy-start.15
  33.2 10.2 copy-start.17
  33.2 10.9 %copy-start.23 = (bf16[32,2,16,128]{3,0,2,1:T(8,128)(2,1)}, bf16[32,2,16,128]{3,0,2,1:T(8,128)(2,1)S(1)}, u32[]{:S(2)}) copy-start(bf16[32,2,16,128]{3,0,2,1:T(8,128)(2,1)S(1)} %get-tuple-element.126) | copy-start | bytes 786436
  38.0 6.4 copy-start.33
  38.0 6.4 copy-start.35
  38.0 6.8 copy-start.19
  38.0 6.8 copy-start.21
  38.1 7.0 copy-start.29
  38.1 7.0 copy-start.31
  45.7 10.8 %collective-permute-start.6 = (bf16[2,32,1,16,128]{4,1,3,2,0:T(8,128)(2,1)S(1)}, bf16[2,32,1,16,128]{4,1,3,2,0:T(8,128)(2,1)S(1)}, u32[]{:S(2)}, u32[]{:S(2)}) collective-permute-start(bf16[2,32,1,16,128]{4,1,3,2,0:T(8,128)(2,1)S(1)} %get-tuple-element.134), channel_id=1, source_target_pairs={{0,64},{64,128},{128,192},{1,65},{65,129},{129,193},{2,66},{66,130... | collective-permute-start | bytes 786440 | tf_op jit(solution)/shard_map/ppermute | solution.py:16
  49.5 11.1 %collective-permute-start.7 = (bf16[2,32,1,16,128]{4,1,3,2,0:T(8,128)(2,1)S(1)}, bf16[2,32,1,16,128]{4,1,3,2,0:T(8,128)(2,1)S(1)}, u32[]{:S(2)}, u32[]{:S(2)}) collective-permute-start(bf16[2,32,1,16,128]{4,1,3,2,0:T(8,128)(2,1)S(1)} %get-tuple-element.135), channel_id=1, source_target_pairs={{64,0},{128,64},{192,128},{65,1},{129,65},{193,129},{66,2},{130,66... | collective-permute-start | bytes 786440 | tf_op jit(solution)/shard_map/ppermute | solution.py:18
  56.5 16.9 %copy-start = (bf16[2,32,1,16,128]{4,1,3,2,0:T(8,128)(2,1)}, bf16[2,32,1,16,128]{4,1,3,2,0:T(8,128)(2,1)S(1)}, u32[]{:S(2)}) copy-start(bf16[2,32,1,16,128]{4,1,3,2,0:T(8,128)(2,1)S(1)} %collective-permute-done.6) | copy-start | bytes 786436
  60.6 12.8 %copy-start.1 = (bf16[2,32,1,16,128]{4,1,3,2,0:T(8,128)(2,1)}, bf16[2,32,1,16,128]{4,1,3,2,0:T(8,128)(2,1)S(1)}, u32[]{:S(2)}) copy-start(bf16[2,32,1,16,128]{4,1,3,2,0:T(8,128)(2,1)S(1)} %collective-permute-done.7) | copy-start | bytes 786436
  60.6 5.4 collective-permute-start.8
  64.0 9.4 collective-permute-start.9
  76.4 7.1 copy-start.72
  76.4 7.2 copy-start.71
  76.4 7.3 copy-start.70
  76.4 8.0 copy-start.69
  76.4 8.7 copy-start.68
  76.4 9.4 copy-start.67
  76.4 10.1 copy-start.66
  76.4 10.8 %copy-start.65 = (bf16[1,1,3,32,32]{3,4,2,1,0:T(8,128)(2,1)S(1)}, bf16[1,1,3,32,32]{3,4,2,1,0:T(8,128)(2,1)}, u32[]{:S(2)}) copy-start(bf16[1,1,3,32,32]{3,4,2,1,0:T(8,128)(2,1)} %get-tuple-element.151) | copy-start | bytes 18436
  76.4 11.5 %copy-start.64 = (bf16[1,1,3,32,32]{3,4,2,1,0:T(8,128)(2,1)S(1)}, bf16[1,1,3,32,32]{3,4,2,1,0:T(8,128)(2,1)}, u32[]{:S(2)}) copy-start(bf16[1,1,3,32,32]{3,4,2,1,0:T(8,128)(2,1)} %get-tuple-element.152) | copy-start | bytes 18436
  77.3 12.3 %collective-permute-start.11 = (bf16[2,32,4,18,1]{1,2,4,3,0:T(4,128)(2,1)S(1)}, bf16[2,32,4,18,1]{1,2,4,3,0:T(4,128)(2,1)}, u32[]{:S(2)}, u32[]{:S(2)}) collective-permute-start(bf16[2,32,4,18,1]{1,2,4,3,0:T(4,128)(2,1)S(1)} %copy.163), channel_id=1, source_target_pairs={{1,0},{2,1},{3,2},{4,3},{5,4},{6,5},{7,6},{9,8},{10,9},{11,10},{12... | collective-permute-start | bytes 27656 | tf_op jit(solution)/shard_map/ppermute | solution.py:18
  78.6 10.0 collective-permute-start.10
  109.9 8.0 collective-permute-start.12
  112.8 8.2 collective-permute-start.13
  121.0 12.4 %collective-permute-start.14 = (bf16[32,4,1,128]{3,0,2,1:T(8,128)(2,1)S(1)}, bf16[32,4,1,128]{3,0,2,1:T(8,128)(2,1)S(1)}, u32[]{:S(2)}, u32[]{:S(2)}) collective-permute-start(bf16[32,4,1,128]{3,0,2,1:T(8,128)(2,1)S(1)} %get-tuple-element.132), channel_id=1, source_target_pairs={{0,8},{8,16},{16,24},{24,32},{32,40},{40,48},{48,56},{1,9},{9,17},... | collective-permute-start | bytes 98312 | tf_op jit(solution)/shard_map/ppermute | solution.py:16
  131.0 5.8 collective-permute-start.15
  138.1 6.0 collective-permute-start.17
  139.4 4.2 collective-permute-start.16
  162.1 75.4 %copy-start.7 = (bf16[3,3,3,32,32]{4,3,2,1,0:T(8,128)(2,1)S(1)}, bf16[3,3,3,32,32]{4,3,2,1,0:T(8,128)(2,1)}, u32[]{:S(2)}) copy-start(bf16[3,3,3,32,32]{4,3,2,1,0:T(8,128)(2,1)} %param.8) | copy-start | bytes 165892
  163.1 74.6 %copy-start.8 = (bf16[3,3,3,32,32]{4,3,2,1,0:T(8,128)(2,1)S(1)}, bf16[3,3,3,32,32]{4,3,2,1,0:T(8,128)(2,1)}, u32[]{:S(2)}) copy-start(bf16[3,3,3,32,32]{4,3,2,1,0:T(8,128)(2,1)} %param.9) | copy-start | bytes 165892
  163.2 848.0 %all-reduce.5.cloned.1.call-start = ((), (), s32[]{:S(2)}) async-start(), calls=%async_computation | async-start | bytes 2359296 | tf_op jit(solution)/shard_map/psum | solution.py:116
  (79 other events, 130.3 us)
Sparse Core Ops, SparseCore 0:
  163.3 74.1 all-reduce.6
  240.2 770.8 all-reduce.4
